TPU v7x, 32 devices: a whole 2x2x4 slice. The times are simulated.
32 devices in a mesh: seq: 8 (over z, x), head: 4 (over y, core).
Axes of the slice: x: 2, y: 2, z: 4, core: 2. Of those that a mesh axis runs over, the one named last changes fastest.
Arguments:
- queries: bfloat16 [2, 512, 8192], P(None, 'seq', 'head'), may hold values from -256 to 256
- keys: bfloat16 [2, 2048, 1024], P(None, 'seq', 'head'), may hold values from -12 to 12
- lengths: int32 [2], replicated, may hold values from 768 to 2048, as said below
- starts: int32 [2], replicated, may hold values from 0 to 256, as said below
Outputs:
- key_scores: float32 [2, 8, 2048], P(None, 'head', 'seq')
- token_scores: float32 [2, 2048], P(None, 'seq')
Inputs may be any that keep to these rules, and one draw needn't show every extreme that they name: `lengths`: every length is a multiple of 128 and at least 768; in every draw one request has length 2048. `starts`: each start is at most its request's length minus 512 minus 128; in every draw one start equals 256.
All inputs are finite; a program needn't handle non-finite values.
Results may differ from a plain program's by a relative error of at most 0.0003.
Values may be sent and summed in bfloat16 or wider, within the bound.
A program may use at most 64 MiB of HBM per device.

v0:
```python
import jax
import jax.numpy as jnp
from jax import lax
from jax.sharding import PartitionSpec as P

H = 64
KVH = 8
D = 128
QLEN = 512


MASK_FILL = -1e30


def body(queries, keys, lengths, starts):
    requests = queries.shape[0]
    query_rows = queries.shape[1]
    heads_local = keys.shape[2] // D
    group_size = H // KVH
    score_scale = D ** (-0.5)
    cycle_index = lax.axis_index("seq")

    def block_scores(query_block, query_pos, shard_piece):
        piece_rows = shard_piece.shape[1]
        key_block = shard_piece.reshape(requests, piece_rows, heads_local, D)
        scores = (
            jnp.einsum(
                "btghd,bkgd->bghtk", query_block, key_block, preferred_element_type=jnp.float32
            )
            * score_scale
        )
        key_pos = jnp.arange(piece_rows, dtype=jnp.int32)
        allowed = (key_pos[None, None, None, None, :] <= query_pos[:, None, None, :, None]) & (
            key_pos[None, None, None, None, :] >= starts[:, None, None, None, None]
        )
        return (jnp.where(allowed, scores, MASK_FILL), allowed)

    own_queries = queries.reshape(requests, query_rows, heads_local, group_size, D)
    query_pos = (
        lengths[:, None]
        - QLEN
        + cycle_index * query_rows
        + jnp.arange(query_rows, dtype=jnp.int32)[None, :]
    )
    stat_shape = (requests, heads_local, group_size, query_rows)
    masked, allowed = block_scores(
        own_queries, query_pos, lax.all_gather(keys, "seq", axis=1, tiled=True)
    )
    new_top = jnp.maximum(
        (jnp.full(stat_shape, MASK_FILL, jnp.float32), jnp.zeros(stat_shape, jnp.float32))[0],
        jnp.max(masked, axis=4),
    )
    added = jnp.sum(jnp.where(allowed, jnp.exp(masked - new_top[..., None]), 0.0), axis=4)
    masked, allowed = block_scores(
        own_queries, query_pos, lax.all_gather(keys, "seq", axis=1, tiled=True)
    )
    probs = jnp.where(allowed, jnp.exp(masked - new_top[..., None]), 0.0) / added[..., None]
    partial_value = jnp.sum(probs, axis=(2, 3))
    key_scores = lax.psum_scatter(partial_value, "seq", scatter_dimension=2, tiled=True)
    token_scores = lax.psum(jnp.sum(key_scores, axis=1), "head")
    return (key_scores, token_scores)


def solution(mesh):
    placed = (P(None, "seq", "head"), P(None, "seq", "head"), P(), P())
    return jax.shard_map(
        body,
        mesh=mesh,
        in_specs=placed,
        out_specs=(P(None, "head", "seq"), P(None, "seq")),
        check_vma=False,
    )
```

profile of v0, /device:TPU:0, one launch (start us, length us, event | category | flops | bytes accessed | tf_op | source)
XLA Modules:
  0.0 167.4 jit_solution(16608121996408399934)
XLA Ops:
  7.2 0.0 all-gather.2.cloned.1.call-start
  7.2 1.8 %copy.10 = bf16[2,256,256]{1,2,0:T(8,128)(2,1)} copy(bf16[2,256,256]{2,1,0:T(8,128)(2,1)} %param.5) | data formatting | bytes 524288 | tf_op args[1]
  9.0 0.0 all-gather.2.cloned.1.call-update
  9.0 0.0 reduce-scatter.4.cloned.1.call-start
  9.1 1.1 copy.19
  10.2 0.7 add_add_fusion
  10.9 0.1 iota_add_fusion
  11.0 0.7 iota_compare_fusion.1
  11.7 0.2 fusion.5
  12.0 51.2 %all-gather.2.cloned.1.call-done = bf16[2,2048,256]{1,2,0:T(8,128)(2,1)} async-done(((bf16[2,256,256]{1,2,0:T(8,128)(2,1)}), bf16[2,2048,256]{1,2,0:T(8,128)(2,1)}) %all-gather.2.cloned.1.call-update) | async-done | bytes 2097168 | tf_op jit(solution)/shard_map/all_gather | solution.py:55
  63.1 0.0 copy-start
  63.1 9.2 %fusion.1 = (f32[2,2,8,64]{3,2,1,0:T(8,128)S(1)}, f32[2,2,2048,64,8]{2,3,4,1,0:T(8,128)}) fusion(pred[2,64,2048]{2,1,0:T(8,128)(4,1)S(1)} %fusion.5, bf16[2,2048,2,128,1]{1,3,4,2,0:T(8,128)(2,1)} %bitcast.31, bf16[2,64,2,8,128]{4,3,2,1,0:T(8,128)(2,1)S(1)} %bitcast.28), kind=kOutput, calls=%fused_computation.4 | convolution fusion | flops 1086322688 | bytes 19668992 | tf_op jit(solution)/shard_map/btghd,bkgd->bghtk/dot_general | solution.py:27
  72.3 0.0 copy-done
  72.3 13.6 %divide_reduce_fusion = f32[2,2,2048]{2,1,0:T(2,128)S(1)} fusion(f32[2,2,8,64]{3,2,1,0:T(8,128)S(1)} %broadcast_maximum_fusion, f32[2,2,2048,64,8]{2,3,4,1,0:T(8,128)} %get-tuple-element.3, pred[2,64,2048]{2,1,0:T(8,128)(4,1)S(1)} %fusion.5, bf16[2,2048,2,128,1]{1,3,4,2,0:T(8,128)(2,1)S(1)} %bitcast.32, bf16[2,64,2,8,128]{4,3,2,1,0:T(8,128)(2,1)S(1)} %bitcast.29), kind=kOutput, calls=%fused_computation.3 | convolution fusion | flops 1115680768 | bytes 19701760 | tf_op jit(solution)/shard_map/div | solution.py:57
  85.9 1.1 copy.16
  87.0 2.1 %reshape.69 = f32[2048,4]{1,0:T(8,128)} reshape(f32[2048,2,2]{2,1,0:T(2,128)S(1)} %bitcast.27) | data formatting | bytes 65536
  89.2 0.0 reduce-scatter.4.cloned.1.call-update
  89.2 62.9 %reduce-scatter.4.cloned.1.call-done = f32[256,4]{1,0:T(8,128)} async-done(((f32[2048,4]{1,0:T(8,128)}), f32[256,4]{1,0:T(8,128)}) %reduce-scatter.4.cloned.1.call-update) | async-done | bytes 4112
  152.1 1.1 reshape.70
  153.2 0.3 bitcast_reduce_fusion
  153.5 0.7 copy.17
  154.2 0.1 copy.18
  154.3 6.2 %psum.7 = f32[2,256]{1,0:T(2,128)} all-reduce(f32[2,256]{1,0:T(2,128)S(1)} %copy.18), channel_id=1, replica_groups=mesh['seq'=8,'head'=4] {'head'}, use_global_device_ids=true, to_apply=%region_5.6 | all-reduce | flops 512 | bytes 4096 | tf_op jit(solution)/shard_map/psum | solution.py:60
  (1 shorter events, 0.0 us)
Async XLA Ops:
  7.2 56.0 %all-gather.2.cloned.1.call-start = ((), (), s32[]{:S(2)}) async-start(), calls=%async_computation.1 | async-start | bytes 2359296 | tf_op jit(solution)/shard_map/all_gather | solution.py:55
  9.0 143.1 %reduce-scatter.4.cloned.1.call-start = ((), (), s32[]{:S(2)}) async-start(), calls=%async_computation.2 | async-start | bytes 1179648
  63.1 9.2 %copy-start = (bf16[2,2048,256]{1,2,0:T(8,128)(2,1)S(1)}, bf16[2,2048,256]{1,2,0:T(8,128)(2,1)}, u32[]{:S(2)}) copy-start(bf16[2,2048,256]{1,2,0:T(8,128)(2,1)} %all-gather.2.cloned.1.call-done) | copy-start | bytes 6291460
Sparse Core Ops, SparseCore 0:
  10.0 53.0 all-gather.1
  89.3 62.7 reduce-scatter.3
where the time goes:
time: 168 us; the launch traced here: 167 us
  waiting for transfers between devices  114 us (68%)
  matrix products  22.8 us (14%)
  between operations  14.1 us (8%)
  local copies, waits for them, and re-layouts  8.06 us (5%)
  blocking collectives  6.21 us (4%)
  other arithmetic  2.06 us (1%)
    unnamed x3, waiting for transfers between devices  62.9 us
    all_gather x1, waiting for transfers between devices, body(): lax.all_gather(keys, 'seq', axis=1, tiled=True)  51.2 us
    div x1, matrix products, body(): jnp.where(allowed, jnp.exp(masked - new_top[..., None]), 0.0)  13.6 us
    dot_general x1, matrix products, block_scores(): jnp.einsum('btghd,bkgd->bghtk', query_block, key_block, preferred_element...  9.18 us
    unnamed x9, local copies, waits for them, and re-layouts  8.06 us
    psum x1, blocking collectives, body(): token_scores = lax.psum(jnp.sum(key_scores, axis=1), 'head')  6.21 us
  transfers between devices with their start and end apart: 2, of which 2 were waited for; matrix products, arithmetic and copies ran while one was open for 2% of the time, Pallas kernels for 0%

commit v1 on v0

v1 whole, which is shorter than its diff:
```python
import functools

import jax
import jax.numpy as jnp
from jax import lax
from jax.experimental import pallas as pl
from jax.experimental.pallas import tpu as pltpu
from jax.sharding import PartitionSpec as P

KVH = 8
D = 128
QLEN = 512
MASK_FILL = -1e30
MASK_FLOOR = -5e29
LOG2E = 1.4426950408889634
MESH = pl.DeviceIdType.MESH


def kernel(
    n_seq, n_head, starts_ref, lengths_ref, q_hbm, k_hbm, key_out, tok_out,
    qs, ks, es, ms, ls, ws, stat, stat_in, cols, cols_in, tok, tok_in,
    q_sem, k_sem, q_send, q_recv, up_send, down_send, k_recv,
    stat_send, stat_recv, col_send, col_recv, tok_send, tok_recv,
):
    requests, tokens, width = q_hbm.shape
    block = k_hbm.shape[1]
    groups = k_hbm.shape[2] // D
    heads = width // (groups * D)
    rows = heads * tokens
    chain = n_seq // 2
    tile = min(256, rows)
    scale = (D ** -0.5) * LOG2E
    me = lax.axis_index("seq")
    head = lax.axis_index("head")
    pair = lax.rem(me, 2)
    spot = me // 2

    def at(seq, hd=None):
        return {"seq": seq, "head": head if hd is None else hd}

    def chain_dev(i):
        return at(i * 2 + pair)

    peer = at(me + 1 - 2 * pair)

    for b in range(requests):
        pltpu.make_async_copy(k_hbm.at[b], ks.at[spot, b], k_sem.at[b]).start()
        for g in range(groups):
            for h in range(heads):
                pltpu.make_async_copy(
                    q_hbm.at[b, :, pl.ds((g * heads + h) * D, D)], qs.at[pair, b, g, h], q_sem.at[b]
                ).start()

    barrier = pltpu.get_barrier_semaphore()
    for d in range(1, chain):
        pl.semaphore_signal(barrier, inc=1, device_id=chain_dev(lax.rem(spot + d, chain)), device_id_type=MESH)
    pl.semaphore_signal(barrier, inc=1, device_id=peer, device_id_type=MESH)
    for d in range(1, n_head):
        pl.semaphore_signal(
            barrier, inc=1, device_id=at(me, lax.rem(head + d, n_head)), device_id_type=MESH
        )
    pl.semaphore_wait(barrier, chain - 1 + 1 + n_head - 1)

    def key_copy(i, b, upward):
        sems = up_send if upward else down_send
        return pltpu.make_async_remote_copy(
            src_ref=ks.at[i, b], dst_ref=ks.at[i, b], send_sem=sems.at[i, b], recv_sem=k_recv.at[i, b],
            device_id=chain_dev(spot + 1 if upward else spot - 1), device_id_type=MESH,
        )

    def send_key(i, b, upward):
        @pl.when((spot < chain - 1) if upward else (spot > 0))
        def _():
            key_copy(i, b, upward).start()

    def query_copy(b):
        return pltpu.make_async_remote_copy(
            src_ref=qs.at[pair, b], dst_ref=qs.at[pair, b], send_sem=q_send.at[b], recv_sem=q_recv.at[b],
            device_id=peer, device_id_type=MESH,
        )

    for b in range(requests):
        pltpu.make_async_copy(k_hbm.at[b], ks.at[spot, b], k_sem.at[b]).wait()
        send_key(spot, b, True)
        send_key(spot, b, False)
    for b in range(requests):
        pltpu.make_async_copy(qs.at[pair, b], qs.at[pair, b], q_sem.at[b]).wait()
        query_copy(b).start()

    def work(i, b, first, count):
        start = starts_ref[b]
        length = lengths_ref[b]
        keypos = (i * 2 + pair) * block + lax.broadcasted_iota(jnp.int32, (block, tile), 0)
        lane_token = lax.rem(lax.broadcasted_iota(jnp.int32, (1, tile), 1), tokens)

        def step(u, carry):
            slot = lax.rem(first + u // groups, 2)
            g = lax.rem(u, groups)
            where = (b * 2 + slot) * groups + g
            k = ks[i, b, :, pl.ds(pl.multiple_of(g * D, D), D)]
            q = qs[slot, b, g].reshape(rows, D)
            pos = length - QLEN + (spot * 2 + slot) * tokens + lane_token
            for r in range(rows // tile):
                s = lax.dot_general(
                    k, q[r * tile:(r + 1) * tile], (((1,), (1,)), ((), ())),
                    preferred_element_type=jnp.float32,
                )
                allowed = (keypos <= pos) & (keypos >= start)
                s = jnp.where(allowed, s, MASK_FILL)
                top = jnp.maximum(jnp.max(s, axis=0, keepdims=True), MASK_FLOOR)
                e = jnp.exp2((s - top) * scale)
                es[i, b, slot, g, :, r * tile:(r + 1) * tile] = e
                ms[i, pl.ds(where, 1), r * tile:(r + 1) * tile] = top
                ls[i, pl.ds(where, 1), r * tile:(r + 1) * tile] = jnp.sum(e, axis=0, keepdims=True)
            return carry

        lax.fori_loop(0, count * groups, step, 0)

    own, other = pair, 1 - pair

    for b in range(requests):
        work(spot, b, own, 1)

    def receive(s, b, count):
        @pl.when(spot - s >= 0)
        def _():
            key_copy(spot - s, b, True).wait_recv()
            send_key(spot - s, b, True)

        @pl.when(spot + s < chain)
        def _():
            key_copy(spot + s, b, False).wait_recv()
            send_key(spot + s, b, False)

        def side(v, carry):
            i = spot - s + v * 2 * s

            @pl.when((i >= 0) & (i < chain))
            def _():
                work(i, b, own, count)

            return carry

        lax.fori_loop(0, 2, side, 0)

    def catch_up(b, reach):
        query_copy(b).wait_recv()

        def one(i, carry):
            work(i, b, other, 1)
            return carry

        lax.fori_loop(jnp.maximum(spot - reach, 0), jnp.minimum(spot + reach, chain - 1) + 1, one, 0)

    last = chain - 1
    for b in range(requests):
        receive(1, b, 1) if last >= 1 else None
    early = min(1, last)
    for b in range(requests - 1):
        catch_up(b, early)

    def middle(s, carry):
        for b in range(requests - 1):
            receive(s, b, 2)
        receive(s, requests - 1, 1)
        return carry

    if last > 1:
        lax.fori_loop(2, last, middle, 0)
        for b in range(requests - 1):
            receive(last, b, 2)
        catch_up(requests - 1, last - 1)
        receive(last, requests - 1, 2)
    else:
        catch_up(requests - 1, last)

    top = ms[0]
    for i in range(1, chain):
        top = jnp.maximum(top, ms[i])
    total = ls[0] * jnp.exp2((ms[0] - top) * scale)
    for i in range(1, chain):
        total += ls[i] * jnp.exp2((ms[i] - top) * scale)
    stat[0] = top
    stat[1] = total
    stat_copy = pltpu.make_async_remote_copy(
        src_ref=stat, dst_ref=stat_in, send_sem=stat_send, recv_sem=stat_recv,
        device_id=peer, device_id_type=MESH,
    )
    stat_copy.start()
    stat_copy.wait()
    full_top = jnp.maximum(stat[0], stat_in[0])
    full = stat[1] * jnp.exp2((stat[0] - full_top) * scale) + stat_in[1] * jnp.exp2(
        (stat_in[0] - full_top) * scale
    )
    inverse = 1.0 / full
    for i in range(chain):
        weight = jnp.exp2((ms[i] - full_top) * scale) * inverse
        for u in range(weight.shape[0]):
            ws[i, u] = weight[u:u + 1]

    ones = jnp.ones((8, 128 if rows >= 128 else rows), jnp.float32)
    lanes = min(128, rows)

    def col_copy(i):
        return pltpu.make_async_remote_copy(
            src_ref=cols.at[i], dst_ref=cols_in.at[spot], send_sem=col_send.at[i], recv_sem=col_recv.at[spot],
            device_id=chain_dev(i), device_id_type=MESH,
        )

    def col_arrival(i):
        return pltpu.make_async_remote_copy(
            src_ref=cols.at[i], dst_ref=cols_in.at[i], send_sem=col_send.at[i], recv_sem=col_recv.at[i],
            device_id=chain_dev(i), device_id_type=MESH,
        )

    def columns(d, carry):
        i = lax.rem(spot + d, chain)

        def one(u, carry):
            b = u // groups
            g = lax.rem(u, groups)
            acc = jnp.zeros((block, lanes), jnp.float32)
            for slot in range(2):
                where = (b * 2 + slot) * groups + g
                for r in range(rows // lanes):
                    w = ws[i, where, :, r * lanes:(r + 1) * lanes]
                    acc += es[i, b, slot, g, :, r * lanes:(r + 1) * lanes] * w
            summed = lax.dot_general(
                ones, acc, (((1,), (1,)), ((), ())), preferred_element_type=jnp.float32,
                precision=lax.Precision.HIGHEST,
            )
            cols[i, pl.ds(u, 1), :] = summed[0:1]
            return carry

        lax.fori_loop(0, requests * groups, one, 0)

        @pl.when(i != spot)
        def _():
            col_copy(i).start()

        return carry

    lax.fori_loop(1, chain + 1, columns, 0)

    def gather(d, acc):
        i = lax.rem(spot + d, chain)
        col_arrival(i).wait_recv()
        return acc + cols_in[i]

    result = lax.fori_loop(1, chain, gather, cols[spot])
    for b in range(requests):
        key_out[b] = result[b * groups:(b + 1) * groups]
        t = result[b * groups:b * groups + 1]
        for g in range(1, groups):
            t += result[b * groups + g:b * groups + g + 1]
        tok[b:b + 1, :] = t

    tok_copies = []
    for d in range(1, n_head):
        tok_copies.append(
            pltpu.make_async_remote_copy(
                src_ref=tok, dst_ref=tok_in.at[d], send_sem=tok_send.at[d], recv_sem=tok_recv.at[d],
                device_id=at(me, lax.rem(head + d, n_head)), device_id_type=MESH,
            )
        )
    for c in tok_copies:
        c.start()
    for c in tok_copies:
        c.wait_recv()
    tok_in[0] = tok[...]
    def head_sum(h, acc):
        return acc + tok_in[lax.rem(head - h + n_head, n_head)]

    tok_out[...] = lax.fori_loop(0, n_head, head_sum, jnp.zeros(tok.shape, jnp.float32))

    for c in tok_copies:
        c.wait_send()
    for d in range(1, chain):
        col_copy(lax.rem(spot + d, chain)).wait_send()
    for b in range(requests):
        query_copy(b).wait_send()

        def sent(i, carry):
            @pl.when((i <= spot) & (spot < chain - 1))
            def _():
                key_copy(i, b, True).wait_send()

            @pl.when((i >= spot) & (spot > 0))
            def _():
                key_copy(i, b, False).wait_send()

            return carry

        lax.fori_loop(0, chain, sent, 0)


def body(n_seq, n_head, queries, keys, lengths, starts):
    requests, tokens, width = queries.shape
    block = keys.shape[1]
    groups = keys.shape[2] // D
    heads = width // (groups * D)
    rows = heads * tokens
    chain = n_seq // 2
    units = requests * 2 * groups
    f32 = jnp.float32
    dma = pltpu.SemaphoreType.DMA
    any_spec = pl.BlockSpec(memory_space=pl.ANY)
    smem = pl.BlockSpec(memory_space=pltpu.SMEM)
    vmem = pl.BlockSpec(memory_space=pltpu.VMEM)
    return pl.pallas_call(
        functools.partial(kernel, n_seq, n_head),
        out_shape=(
            jax.ShapeDtypeStruct((requests, groups, block), f32),
            jax.ShapeDtypeStruct((requests, block), f32),
        ),
        in_specs=[smem, smem, any_spec, any_spec],
        out_specs=(vmem, vmem),
        scratch_shapes=[
            pltpu.VMEM((2, requests, groups, heads, tokens, D), queries.dtype),
            pltpu.VMEM((chain, requests, block, groups * D), keys.dtype),
            pltpu.VMEM((chain, requests, 2, groups, block, rows), f32),
            pltpu.VMEM((chain, units, rows), f32),
            pltpu.VMEM((chain, units, rows), f32),
            pltpu.VMEM((chain, units, 1, rows), f32),
            pltpu.VMEM((2, units, rows), f32),
            pltpu.VMEM((2, units, rows), f32),
            pltpu.VMEM((chain, requests * groups, block), f32),
            pltpu.VMEM((chain, requests * groups, block), f32),
            pltpu.VMEM((requests, block), f32),
            pltpu.VMEM((n_head, requests, block), f32),
            dma((requests,)), dma((requests,)), dma((requests,)), dma((requests,)),
            dma((chain, requests)), dma((chain, requests)), dma((chain, requests)),
            dma, dma, dma((chain,)), dma((chain,)), dma((n_head,)), dma((n_head,)),
        ],
        compiler_params=pltpu.CompilerParams(
            collective_id=0, has_side_effects=True, vmem_limit_bytes=60 * 1024 * 1024
        ),
    )(starts, lengths, queries, keys)


def solution(mesh):
    placed = (P(None, "seq", "head"), P(None, "seq", "head"), P(), P())
    return jax.shard_map(
        functools.partial(body, mesh.shape["seq"], mesh.shape["head"]),
        mesh=mesh,
        in_specs=placed,
        out_specs=(P(None, "head", "seq"), P(None, "seq")),
        check_vma=False,
    )
```

time: 168 us -> 41.7 us (0.25)
  waiting for transfers between devices: 114 us -> 0 us
  Pallas kernels: 0 us -> 39.1 us
  matrix products: 22.8 us -> 0 us
  between operations: 14.1 us -> 0.65 us
  local copies, waits for them, and re-layouts: 8.06 us -> 1.85 us
  blocking collectives: 6.21 us -> 0 us
  other arithmetic: 2.06 us -> 0 us
    unnamed x3 -> x0, waiting for transfers between devices: 62.9 us -> none
    all_gather x1 -> x0, waiting for transfers between devices: 51.2 us -> none  [body(): lax.all_gather(keys, 'seq', axis=1, tiled=True)]
    pallas_call x0 -> x1, Pallas kernels: none -> 39.1 us  [body(): pl.pallas_call(functools.partial(kernel, n_seq, n_head), out_shape=(jax.S...]
    div x1 -> x0, matrix products: 13.6 us -> none  [body(): jnp.where(allowed, jnp.exp(masked - new_top[..., None]), 0.0)]
    dot_general x1 -> x0, matrix products: 9.18 us -> none  [block_scores(): jnp.einsum('btghd,bkgd->bghtk', query_block, key_block, preferred_element...]
    psum x1 -> x0, blocking collectives: 6.21 us -> none  [body(): token_scores = lax.psum(jnp.sum(key_scores, axis=1), 'head')]
    unnamed x9 -> x4, local copies, waits for them, and re-layouts: 8.06 us -> 1.85 us
  transfers between devices with their start and end apart: 2 -> 0, of which waited for: 2 -> 0; matrix products, arithmetic and copies ran while one was open for 2% -> 0% of each run, Pallas kernels for 0% -> 0%
where the time goes in v1:
time: 41.7 us; the launch traced here: 41.6 us
  Pallas kernels  39.1 us (94%)
  local copies, waits for them, and re-layouts  1.85 us (4%)
  between operations  0.65 us (2%)
    pallas_call x1, Pallas kernels, body(): pl.pallas_call(functools.partial(kernel, n_seq, n_head), out_shape=(jax.S...  39.1 us
    unnamed x4, local copies, waits for them, and re-layouts  1.85 us

profile of v1, /device:TPU:0, one launch (start us, length us, event | category | flops | bytes accessed | tf_op | source)
XLA Modules:
  0.0 41.6 jit_solution(9915955139877367167)
XLA Ops:
  0.6 39.1 %shard_map.59 = (f32[2,2,256]{2,1,0:T(2,128)}, f32[2,256]{1,0:T(2,128)}) custom-call(s32[2]{0:T(128)} %starts_ref.1, s32[2]{0:T(128)} %lengths_ref.1, bf16[2,64,2048]{2,1,0:T(8,128)(2,1)} %q_hbm.1, bf16[2,256,256]{2,1,0:T(8,128)(2,1)} %k_hbm.1), custom_call_target="tpu_custom_call" | custom-call | tf_op jit(solution)/shard_map/pallas_call | solution.py:310
  39.7 0.0 copy-start
  39.7 1.3 %copy.8 = f32[2,2,256]{2,1,0:T(2,128)} copy(f32[2,2,256]{2,1,0:T(2,128)} %get-tuple-element.4) | data formatting | bytes 8192
  41.0 0.0 copy-done
  41.0 0.6 %copy.9 = f32[2,256]{1,0:T(2,128)} copy(f32[2,256]{1,0:T(2,128)S(1)} %copy-done) | data formatting | bytes 4096
Async XLA Ops:
  39.7 1.3 %copy-start = (f32[2,256]{1,0:T(2,128)S(1)}, f32[2,256]{1,0:T(2,128)}, u32[]{:S(2)}) copy-start(f32[2,256]{1,0:T(2,128)} %get-tuple-element.5) | copy-start | bytes 6148

commit v2 on v0

v2 whole, which is shorter than its diff:
```python
import functools

import jax
import jax.numpy as jnp
from jax import lax
from jax.experimental import pallas as pl
from jax.experimental.pallas import tpu as pltpu
from jax.sharding import PartitionSpec as P

KVH = 8
D = 128
QLEN = 512
MASK_FILL = -1e30
MASK_FLOOR = -5e29
LOG2E = 1.4426950408889634
MESH = pl.DeviceIdType.MESH


def kernel(
    n_seq, n_head, starts_ref, lengths_ref, q_hbm, k_hbm, key_out, tok_out,
    qs, ks, es, ms, ls, ws, stat, stat_in, cols, cols_in, tok, tok_in,
    q_sem, k_sem, q_send, q_recv, up_send, down_send, k_recv,
    stat_send, stat_recv, col_send, col_recv, tok_send, tok_recv,
):
    requests, tokens, width = q_hbm.shape
    block = k_hbm.shape[1]
    groups = k_hbm.shape[2] // D
    heads = width // (groups * D)
    rows = heads * tokens
    items = requests * groups
    chain = n_seq // 2
    last = chain - 1
    tile = min(256, rows)
    lanes = min(128, rows)
    scale = (D ** -0.5) * LOG2E
    me = lax.axis_index("seq")
    head = lax.axis_index("head")
    pair = lax.rem(me, 2)
    spot = me // 2
    own, other = pair, 1 - pair

    def at(seq, hd=None):
        return {"seq": seq, "head": head if hd is None else hd}

    def chain_dev(i, hd=None):
        return at(i * 2 + pair, hd)

    def head_at(d):
        return lax.rem(head + d, n_head)

    peer = at(me + 1 - 2 * pair)

    def key_load(u):
        b, g = divmod(u, groups)
        return pltpu.make_async_copy(k_hbm.at[b, :, pl.ds(g * D, D)], ks.at[spot, u], k_sem.at[u])

    for u in range(items):
        key_load(u).start()
    for u in range(items):
        b, g = divmod(u, groups)
        for h in range(heads):
            pltpu.make_async_copy(
                q_hbm.at[b, :, pl.ds((g * heads + h) * D, D)], qs.at[pair, u, h], q_sem.at[u]
            ).start()

    barrier = pltpu.get_barrier_semaphore()

    def greet(device):
        pl.semaphore_signal(barrier, inc=1, device_id=device, device_id_type=MESH)

    @pl.when(spot > 0)
    def _():
        greet(chain_dev(spot - 1))

    @pl.when(spot < last)
    def _():
        greet(chain_dev(spot + 1))

    greet(peer)
    for d in range(1, n_head):
        greet(at(me, head_at(d)))
    inner = jnp.where(spot > 0, 1, 0) + jnp.where(spot < last, 1, 0)
    pl.semaphore_wait(barrier, inner + n_head)

    def key_copy(i, u, upward):
        sems = up_send if upward else down_send
        return pltpu.make_async_remote_copy(
            src_ref=ks.at[i, u], dst_ref=ks.at[i, u], send_sem=sems.at[i, u], recv_sem=k_recv.at[i, u],
            device_id=chain_dev(spot + 1 if upward else spot - 1), device_id_type=MESH,
        )

    def send_key(i, u, upward):
        @pl.when((spot < last) if upward else (spot > 0))
        def _():
            key_copy(i, u, upward).start()

    def query_copy(u):
        return pltpu.make_async_remote_copy(
            src_ref=qs.at[pair, u], dst_ref=qs.at[pair, u], send_sem=q_send.at[u], recv_sem=q_recv.at[u],
            device_id=peer, device_id_type=MESH,
        )

    for u in range(items):
        key_load(u).wait()
        send_key(spot, u, True)
        send_key(spot, u, False)
    for u in range(items):
        pltpu.make_async_copy(qs.at[pair, u], qs.at[pair, u], q_sem.at[u]).wait()
        query_copy(u).start()

    lane_token = lax.rem(lax.broadcasted_iota(jnp.int32, (1, tile), 1), tokens)
    key_row = lax.broadcasted_iota(jnp.int32, (block, 1), 0)

    def work(i, u, first, count):
        start = starts_ref[u // groups]
        length = lengths_ref[u // groups]
        keypos = (i * 2 + pair) * block + key_row
        keypos = jnp.where(keypos >= start, keypos, 2 ** 30)
        k = ks[i, u]

        def step(v, carry):
            slot = lax.rem(first + v, 2)
            q = qs[slot, u].reshape(rows, D)
            pos = length - QLEN + (spot * 2 + slot) * tokens + lane_token
            for r in range(rows // tile):
                part = slice(r * tile, (r + 1) * tile)
                s = lax.dot_general(
                    k, q[part], (((1,), (1,)), ((), ())), preferred_element_type=jnp.float32
                )
                s = jnp.where(keypos <= pos, s, MASK_FILL)
                top = jnp.maximum(jnp.max(s, axis=0, keepdims=True), MASK_FLOOR)
                e = jnp.exp2((s - top) * scale)
                es[i, u, slot, :, part] = e
                ms[i, u, pl.ds(slot, 1), part] = top
                ls[i, u, pl.ds(slot, 1), part] = jnp.sum(e, axis=0, keepdims=True)
            return carry

        lax.fori_loop(0, count, step, 0)

    def arrive(s, u):
        @pl.when(spot - s >= 0)
        def _():
            key_copy(spot - s, u, True).wait_recv()
            send_key(spot - s, u, True)

        @pl.when(spot + s < chain)
        def _():
            key_copy(spot + s, u, False).wait_recv()
            send_key(spot + s, u, False)

    def sides(s, u, count):
        def side(v, carry):
            i = spot - s + v * 2 * s

            @pl.when((i >= 0) & (i < chain))
            def _():
                work(i, u, own, count)

            return carry

        lax.fori_loop(0, 2, side, 0)

    def catch_up(u, reach):
        query_copy(u).wait_recv()

        def one(i, carry):
            work(i, u, other, 1)
            return carry

        lax.fori_loop(jnp.maximum(spot - reach, 0), jnp.minimum(spot + reach, last) + 1, one, 0)

    def stat_copy(u):
        return pltpu.make_async_remote_copy(
            src_ref=stat.at[u], dst_ref=stat_in.at[u], send_sem=stat_send.at[u], recv_sem=stat_recv.at[u],
            device_id=peer, device_id_type=MESH,
        )

    def summarize(u):
        top = ms[0, u]
        for i in range(1, chain):
            top = jnp.maximum(top, ms[i, u])
        total = ls[0, u] * jnp.exp2((ms[0, u] - top) * scale)
        for i in range(1, chain):
            total += ls[i, u] * jnp.exp2((ms[i, u] - top) * scale)
        stat[u, 0] = top
        stat[u, 1] = total
        stat_copy(u).start()

    def col_copy(i, b):
        return pltpu.make_async_remote_copy(
            src_ref=cols.at[i, b], dst_ref=cols_in.at[spot, b], send_sem=col_send.at[i, b],
            recv_sem=col_recv.at[spot, b], device_id=chain_dev(i), device_id_type=MESH,
        )

    def tok_copy(i, d, b):
        return pltpu.make_async_remote_copy(
            src_ref=tok.at[i, b], dst_ref=tok_in.at[spot, d, b], send_sem=tok_send.at[i, d, b],
            recv_sem=tok_recv.at[spot, d, b], device_id=chain_dev(i, head_at(d)), device_id_type=MESH,
        )

    ones = jnp.ones((8, lanes), jnp.float32)

    def finish(u):
        b, g = divmod(u, groups)
        stat_copy(u).wait_recv()
        full_top = jnp.maximum(stat[u, 0], stat_in[u, 0])
        full = stat[u, 1] * jnp.exp2((stat[u, 0] - full_top) * scale) + stat_in[u, 1] * jnp.exp2(
            (stat_in[u, 0] - full_top) * scale
        )
        inverse = 1.0 / full
        for i in range(chain):
            weight = jnp.exp2((ms[i, u] - full_top) * scale) * inverse
            for slot in range(2):
                ws[i, slot] = weight[slot:slot + 1]

        def columns(d, carry):
            i = lax.rem(spot + d, chain)
            acc = jnp.zeros((block, lanes), jnp.float32)
            for slot in range(2):
                for r in range(rows // lanes):
                    part = slice(r * lanes, (r + 1) * lanes)
                    acc += es[i, u, slot, :, part] * ws[i, slot, :, part]
            summed = lax.dot_general(
                ones, acc, (((1,), (1,)), ((), ())), preferred_element_type=jnp.float32,
                precision=lax.Precision.HIGHEST,
            )[0:1]
            cols[i, b, g:g + 1, :] = summed
            if g == groups - 1:
                for other_g in range(groups - 1):
                    summed = cols[i, b, other_g:other_g + 1, :] + summed
                tok[i, b] = summed

                @pl.when(i != spot)
                def _():
                    col_copy(i, b).start()

                for h in range(1, n_head):
                    tok_copy(i, h, b).start()
            return carry

        lax.fori_loop(1, chain + 1, columns, 0)

    def closing(u):
        summarize(u)
        if u > 0:
            finish(u - 1)

    def stage(s, caught, final):
        for u in range(items):
            arrive(s, u)
            if caught:
                catch_up(u, s - 1)
            sides(s, u, 2 if s >= 2 or caught else 1)
            if final:
                closing(u)

    for u in range(items):
        work(spot, u, own, 1)
    if last == 0:
        for u in range(items):
            catch_up(u, 0)
            closing(u)
    if last >= 1:
        stage(1, last == 1, last == 1)
    if last >= 2:
        stage(2, True, last == 2)
    if last >= 3:
        def middle(s, carry):
            for u in range(items):
                arrive(s, u)
                sides(s, u, 2)
            return carry

        lax.fori_loop(3, last, middle, 0)
        stage(last, False, True)
    finish(items - 1)

    for b in range(requests):
        cols_in[spot, b] = cols[spot, b]

        def landed(i, carry):
            @pl.when(i != spot)
            def _():
                col_arrival = pltpu.make_async_remote_copy(
                    src_ref=cols.at[i, b], dst_ref=cols_in.at[i, b], send_sem=col_send.at[i, b],
                    recv_sem=col_recv.at[i, b], device_id=chain_dev(i), device_id_type=MESH,
                )
                col_arrival.wait_recv()

            for d in range(1, n_head):
                tok_arrival = pltpu.make_async_remote_copy(
                    src_ref=tok.at[i, b], dst_ref=tok_in.at[i, d, b], send_sem=tok_send.at[i, d, b],
                    recv_sem=tok_recv.at[i, d, b], device_id=chain_dev(i, head_at(d)), device_id_type=MESH,
                )
                tok_arrival.wait_recv()
            return carry

        lax.fori_loop(0, chain, landed, 0)

        def gather(i, acc):
            return acc + cols_in[i, b]

        key_out[b] = lax.fori_loop(1, chain, gather, cols_in[0, b])
        for i in range(chain):
            part = cols_in[i, b, groups - 1:groups, :]
            for g in range(groups - 1):
                part = cols_in[i, b, g:g + 1, :] + part
            tok_in[i, 0, b] = part

        def head_sum(h, acc):
            d = lax.rem(head - h + n_head, n_head)
            for i in range(chain):
                acc = acc + tok_in[i, d, b]
            return acc

        tok_out[b:b + 1, :] = lax.fori_loop(0, n_head, head_sum, jnp.zeros((1, block), jnp.float32))

    def sent(i, carry):
        for b in range(requests):
            @pl.when(i != spot)
            def _():
                col_copy(i, b).wait_send()

            for d in range(1, n_head):
                tok_copy(i, d, b).wait_send()
        for u in range(items):
            @pl.when((i <= spot) & (spot < last))
            def _():
                key_copy(i, u, True).wait_send()

            @pl.when((i >= spot) & (spot > 0))
            def _():
                key_copy(i, u, False).wait_send()

        return carry

    lax.fori_loop(0, chain, sent, 0)
    for u in range(items):
        query_copy(u).wait_send()
        stat_copy(u).wait_send()


def body(n_seq, n_head, queries, keys, lengths, starts):
    requests, tokens, width = queries.shape
    block = keys.shape[1]
    groups = keys.shape[2] // D
    heads = width // (groups * D)
    rows = heads * tokens
    chain = n_seq // 2
    items = requests * groups
    f32 = jnp.float32
    dma = pltpu.SemaphoreType.DMA
    any_spec = pl.BlockSpec(memory_space=pl.ANY)
    smem = pl.BlockSpec(memory_space=pltpu.SMEM)
    vmem = pl.BlockSpec(memory_space=pltpu.VMEM)
    return pl.pallas_call(
        functools.partial(kernel, n_seq, n_head),
        out_shape=(
            jax.ShapeDtypeStruct((requests, groups, block), f32),
            jax.ShapeDtypeStruct((requests, block), f32),
        ),
        in_specs=[smem, smem, any_spec, any_spec],
        out_specs=(vmem, vmem),
        scratch_shapes=[
            pltpu.VMEM((2, items, heads, tokens, D), queries.dtype),
            pltpu.VMEM((chain, items, block, D), keys.dtype),
            pltpu.VMEM((chain, items, 2, block, rows), f32),
            pltpu.VMEM((chain, items, 2, rows), f32),
            pltpu.VMEM((chain, items, 2, rows), f32),
            pltpu.VMEM((chain, 2, 1, rows), f32),
            pltpu.VMEM((items, 2, 2, rows), f32),
            pltpu.VMEM((items, 2, 2, rows), f32),
            pltpu.VMEM((chain, requests, groups, block), f32),
            pltpu.VMEM((chain, requests, groups, block), f32),
            pltpu.VMEM((chain, requests, 1, block), f32),
            pltpu.VMEM((chain, n_head, requests, 1, block), f32),
            dma((items,)), dma((items,)), dma((items,)), dma((items,)),
            dma((chain, items)), dma((chain, items)), dma((chain, items)),
            dma((items,)), dma((items,)), dma((chain, requests)), dma((chain, requests)),
            dma((chain, n_head, requests)), dma((chain, n_head, requests)),
        ],
        compiler_params=pltpu.CompilerParams(
            collective_id=0, has_side_effects=True, vmem_limit_bytes=60 * 1024 * 1024
        ),
    )(starts, lengths, queries, keys)


def solution(mesh):
    placed = (P(None, "seq", "head"), P(None, "seq", "head"), P(), P())
    return jax.shard_map(
        functools.partial(body, mesh.shape["seq"], mesh.shape["head"]),
        mesh=mesh,
        in_specs=placed,
        out_specs=(P(None, "head", "seq"), P(None, "seq")),
        check_vma=False,
    )
```

time: 168 us -> 39.6 us (0.24)
  waiting for transfers between devices: 114 us -> 0 us
  Pallas kernels: 0 us -> 37 us
  matrix products: 22.8 us -> 0 us
  between operations: 14.1 us -> 0.65 us
  local copies, waits for them, and re-layouts: 8.06 us -> 1.85 us
  blocking collectives: 6.21 us -> 0 us
  other arithmetic: 2.06 us -> 0 us
    unnamed x3 -> x0, waiting for transfers between devices: 62.9 us -> none
    all_gather x1 -> x0, waiting for transfers between devices: 51.2 us -> none  [body(): lax.all_gather(keys, 'seq', axis=1, tiled=True)]
    pallas_call x0 -> x1, Pallas kernels: none -> 37 us  [body(): pl.pallas_call(functools.partial(kernel, n_seq, n_head), out_shape=(jax.S...]
    div x1 -> x0, matrix products: 13.6 us -> none  [body(): jnp.where(allowed, jnp.exp(masked - new_top[..., None]), 0.0)]
    dot_general x1 -> x0, matrix products: 9.18 us -> none  [block_scores(): jnp.einsum('btghd,bkgd->bghtk', query_block, key_block, preferred_element...]
    psum x1 -> x0, blocking collectives: 6.21 us -> none  [body(): token_scores = lax.psum(jnp.sum(key_scores, axis=1), 'head')]
    unnamed x9 -> x4, local copies, waits for them, and re-layouts: 8.06 us -> 1.85 us
  transfers between devices with their start and end apart: 2 -> 0, of which waited for: 2 -> 0; matrix products, arithmetic and copies ran while one was open for 2% -> 0% of each run, Pallas kernels for 0% -> 0%
where the time goes in v2:
time: 39.6 us; the launch traced here: 39.5 us
  Pallas kernels  37 us (93%)
  local copies, waits for them, and re-layouts  1.85 us (5%)
  between operations  0.65 us (2%)
    pallas_call x1, Pallas kernels, body(): pl.pallas_call(functools.partial(kernel, n_seq, n_head), out_shape=(jax.S...  37 us
    unnamed x4, local copies, waits for them, and re-layouts  1.85 us

profile of v2, /device:TPU:0, one launch (start us, length us, event | category | flops | bytes accessed | tf_op | source)
XLA Modules:
  0.0 39.5 jit_solution(11534372469202689364)
XLA Ops:
  0.6 37.0 %shard_map.59 = (f32[2,2,256]{2,1,0:T(2,128)}, f32[2,256]{1,0:T(2,128)}) custom-call(s32[2]{0:T(128)} %starts_ref.1, s32[2]{0:T(128)} %lengths_ref.1, bf16[2,64,2048]{2,1,0:T(8,128)(2,1)} %q_hbm.1, bf16[2,256,256]{2,1,0:T(8,128)(2,1)} %k_hbm.1), custom_call_target="tpu_custom_call" | custom-call | tf_op jit(solution)/shard_map/pallas_call | solution.py:356
  37.6 0.0 copy-start
  37.6 1.3 %copy.8 = f32[2,2,256]{2,1,0:T(2,128)} copy(f32[2,2,256]{2,1,0:T(2,128)} %get-tuple-element.4) | data formatting | bytes 8192
  38.9 0.0 copy-done
  38.9 0.6 %copy.9 = f32[2,256]{1,0:T(2,128)} copy(f32[2,256]{1,0:T(2,128)S(1)} %copy-done) | data formatting | bytes 4096
Async XLA Ops:
  37.6 1.3 %copy-start = (f32[2,256]{1,0:T(2,128)S(1)}, f32[2,256]{1,0:T(2,128)}, u32[]{:S(2)}) copy-start(f32[2,256]{1,0:T(2,128)} %get-tuple-element.5) | copy-start | bytes 6148

commit v3 on v2

--- a/solution.py
+++ b/solution.py
@@ -17,7 +17,7 @@
 
 
 def kernel(
-    n_seq, n_head, starts_ref, lengths_ref, q_hbm, k_hbm, key_out, tok_out,
+    n_seq, n_head, starts_ref, lengths_ref, q_hbm, k_hbm, packed_out,
     qs, ks, es, ms, ls, ws, stat, stat_in, cols, cols_in, tok, tok_in,
     q_sem, k_sem, q_send, q_recv, up_send, down_send, k_recv,
     stat_send, stat_recv, col_send, col_recv, tok_send, tok_recv,
@@ -214,7 +214,7 @@
                 ws[i, slot] = weight[slot:slot + 1]
 
         def columns(d, carry):
-            i = lax.rem(spot + d, chain)
+            i = jnp.where(2 * spot < chain, last - d, d)
             acc = jnp.zeros((block, lanes), jnp.float32)
             for slot in range(2):
                 for r in range(rows // lanes):
@@ -238,7 +238,7 @@
                     tok_copy(i, h, b).start()
             return carry
 
-        lax.fori_loop(1, chain + 1, columns, 0)
+        lax.fori_loop(0, chain, columns, 0)
 
     def closing(u):
         summarize(u)
@@ -300,7 +300,7 @@
         def gather(i, acc):
             return acc + cols_in[i, b]
 
-        key_out[b] = lax.fori_loop(1, chain, gather, cols_in[0, b])
+        packed_out[b * groups:(b + 1) * groups, :] = lax.fori_loop(1, chain, gather, cols_in[0, b])
         for i in range(chain):
             part = cols_in[i, b, groups - 1:groups, :]
             for g in range(groups - 1):
@@ -313,7 +313,7 @@
                 acc = acc + tok_in[i, d, b]
             return acc
 
-        tok_out[b:b + 1, :] = lax.fori_loop(0, n_head, head_sum, jnp.zeros((1, block), jnp.float32))
+        packed_out[items + b:items + b + 1, :] = lax.fori_loop(0, n_head, head_sum, jnp.zeros((1, block), jnp.float32))
 
     def sent(i, carry):
         for b in range(requests):
@@ -353,14 +353,11 @@
     any_spec = pl.BlockSpec(memory_space=pl.ANY)
     smem = pl.BlockSpec(memory_space=pltpu.SMEM)
     vmem = pl.BlockSpec(memory_space=pltpu.VMEM)
-    return pl.pallas_call(
+    packed = pl.pallas_call(
         functools.partial(kernel, n_seq, n_head),
-        out_shape=(
-            jax.ShapeDtypeStruct((requests, groups, block), f32),
-            jax.ShapeDtypeStruct((requests, block), f32),
-        ),
+        out_shape=jax.ShapeDtypeStruct((items + requests, block), f32),
         in_specs=[smem, smem, any_spec, any_spec],
-        out_specs=(vmem, vmem),
+        out_specs=vmem,
         scratch_shapes=[
             pltpu.VMEM((2, items, heads, tokens, D), queries.dtype),
             pltpu.VMEM((chain, items, block, D), keys.dtype),
@@ -384,6 +381,19 @@
         ),
     )(starts, lengths, queries, keys)
 
+    def unpack(packed_ref, key_ref, tok_ref):
+        for b in range(requests):
+            key_ref[b] = packed_ref[b * groups:(b + 1) * groups]
+        tok_ref[...] = packed_ref[items:]
+
+    return pl.pallas_call(
+        unpack,
+        out_shape=(
+            jax.ShapeDtypeStruct((requests, groups, block), f32),
+            jax.ShapeDtypeStruct((requests, block), f32),
+        ),
+    )(packed)
+
 
 def solution(mesh):
     placed = (P(None, "seq", "head"), P(None, "seq", "head"), P(), P())

time: 39.6 us -> 39.1 us (0.987)
  local copies, waits for them, and re-layouts: 1.85 us -> 0 us
  Pallas kernels: 37 us -> 38.3 us
    unnamed x4 -> x0, local copies, waits for them, and re-layouts: 1.85 us -> none
    pallas_call x1 -> x2, Pallas kernels: 37 us -> 38.3 us  [the longest x1 37 us: body(): pl.pallas_call(functools.partial(kernel, n_seq, n_head), out_shape=jax.Sh...]
where the time goes in v3:
time: 39.1 us; the launch traced here: 38.9 us
  Pallas kernels  38.3 us (98%)
  between operations  0.64 us (2%)
    pallas_call x1, Pallas kernels, body(): pl.pallas_call(functools.partial(kernel, n_seq, n_head), out_shape=jax.Sh...  37 us
    pallas_call x1, Pallas kernels, body(): pl.pallas_call(unpack, out_shape=(jax.ShapeDtypeStruct((requests, groups,...  1.3 us

profile of v3, /device:TPU:0, one launch (start us, length us, event | category | flops | bytes accessed | tf_op | source)
XLA Modules:
  0.0 38.9 jit_solution(10392704770753466372)
XLA Ops:
  0.6 37.0 %shard_map.59.packed_ref = f32[6,256]{1,0:T(8,128)} custom-call(s32[2]{0:T(128)} %starts_ref.1, s32[2]{0:T(128)} %lengths_ref.1, bf16[2,64,2048]{2,1,0:T(8,128)(2,1)} %q_hbm.1, bf16[2,256,256]{2,1,0:T(8,128)(2,1)} %k_hbm.1), custom_call_target="tpu_custom_call" | custom-call | tf_op jit(solution)/shard_map/pallas_call | solution.py:356
  37.6 1.3 %shard_map.60 = (f32[2,2,256]{2,1,0:T(2,128)}, f32[2,256]{1,0:T(2,128)}) custom-call(f32[6,256]{1,0:T(8,128)} %shard_map.59.packed_ref), custom_call_target="tpu_custom_call" | custom-call | tf_op jit(solution)/shard_map/pallas_call | solution.py:389
